TPU v7x, 128 devices: a whole 4x4x4 slice. The times are simulated.
128 devices in a mesh: grp: 2 (over core), dev: 64 (over x, z, y).
Axes of the slice: x: 4, y: 4, z: 4, core: 2. Of those that a mesh axis runs over, the one named last changes fastest.
Arguments:
- state: float32 [2, 24, 24, 16384], P(None, None, None, ('grp', 'dev')), may hold values from -6 to 6
- hamiltonian: float32 [24, 24], replicated, may hold values from -1.2 to 1.2
- mode_rates: float32 [96], replicated, may hold values from 0.05 to 2
- ado_modes: int32 [3, 16384], P(None, ('grp', 'dev')), may hold values from 0 to 96
- link_src: int32 [8, 16384], P(None, ('grp', 'dev')), may hold values from 0 to 383, as said below
- link_site: int32 [8, 16384], P(None, ('grp', 'dev')), may hold values from 0 to 23
- link_coef: float32 [4, 8, 16384], P(None, None, ('grp', 'dev')), may hold values from -2.4 to 2.4
- send_ids: int32 [128, 256], P(('grp', 'dev')), may hold values from 0 to 127
- step_units: int32 [], replicated, may hold values from 12 to 16
Outputs:
- new_state: float32 [2, 24, 24, 16384], P(None, None, None, ('grp', 'dev'))
- error_norm: float32 [], replicated
Inputs may be any that keep to these rules, and one draw needn't show every extreme that they name: `link_src`: on each device every received position 128 to 383 is named by 1 to 4 couplings of that device's matrices, and some position by exactly 4.
All inputs are finite; a program needn't handle non-finite values.
Results may differ from a plain program's by a relative error of at most 0.0003.
Values sent between devices are 32-bit elements; how exact they have to be, the bound alone decides.
No kernel may reach another device: no remote copies, remote signals or barrier semaphores. Data moves between devices by JAX's collectives and lax.ppermute only.
A program may use at most 128 MiB of HBM per device.

v0:
```python
import functools
import jax
import jax.numpy as jnp
from jax import lax
from jax.sharding import Mesh
from jax.sharding import PartitionSpec as P

DEV = ("dev_0", "dev_1", "dev_2")
GRP_DEV = ("grp", "dev_0", "dev_1", "dev_2")
TABLEAU = (
    (0.2,),
    (3.0 / 40, 9.0 / 40),
    (44.0 / 45, -56.0 / 15, 32.0 / 9),
    (19372.0 / 6561, -25360.0 / 2187, 64448.0 / 6561, -212.0 / 729),
    (9017.0 / 3168, -355.0 / 33, 46732.0 / 5247, 49.0 / 176, -5103.0 / 18656),
    (35.0 / 384, 0.0, 500.0 / 1113, 125.0 / 192, -2187.0 / 6784, 11.0 / 84),
)
ERRORS = (71.0 / 57600, 0.0, -71.0 / 16695, 71.0 / 1920, -17253.0 / 339200, 22.0 / 525, -1.0 / 40)
ABS_TOL = 0.001
REL_TOL = 0.01
UNIT_STEP = 1.0 / 64
HIGHEST = lax.Precision.HIGHEST


def one_axis_at_a_time(shard, axes):
    return functools.reduce(lax.psum, axes, shard)


def commute(symmetric, current):
    left_prod = jnp.einsum("ab,sbcx->sacx", symmetric, current, precision=HIGHEST)
    right_prod = jnp.einsum("sabx,bc->sacx", current, symmetric, precision=HIGHEST)
    return left_prod - right_prod


def decay_rates(ado_modes, mode_rates):
    extended = jnp.concatenate([mode_rates, jnp.zeros((1,), mode_rates.dtype)])
    levels = jnp.arange(extended.shape[0], dtype=jnp.int32)
    hits = (ado_modes[:, None, :] == levels[None, :, None]).astype(mode_rates.dtype)
    return jnp.sum(hits * extended[None, :, None], axis=(0, 1))


def selector(indices, count, dtype):
    levels = jnp.arange(count, dtype=jnp.int32)
    return (levels[:, None] == indices.reshape(-1)[None, :]).astype(dtype)


def masked_term(source, sites, coef):
    levels = jnp.arange(source.shape[1], dtype=jnp.int32)
    indicator = (levels[:, None] == sites[None, :]).astype(source.dtype)
    row_mask = indicator[:, None, :]
    column_mask = indicator[None, :, :]
    weight_real = coef[0] * row_mask - coef[2] * column_mask
    weight_imag = coef[1] * row_mask - coef[3] * column_mask
    real_part = weight_real * source[0] - weight_imag * source[1]
    imag_part = weight_real * source[1] + weight_imag * source[0]
    return jnp.stack([imag_part, -real_part])


def shards(
    state, hamiltonian, mode_rates, ado_modes, link_src, link_site, link_coef, send_ids, step_units
):
    outgoing = send_ids[0]
    symmetric = 0.5 * (hamiltonian + hamiltonian.T)
    decay = decay_rates(ado_modes, mode_rates)
    step_size = step_units.astype(state.dtype) * UNIT_STEP
    groups = lax.axis_size("grp")
    members = lax.axis_size(DEV)
    sites = state.shape[1]
    owned = state.shape[3]
    received = outgoing.shape[0]
    links = link_src.shape[0]
    flat_rows = 2 * sites * sites
    pack_table = selector(outgoing, owned, state.dtype)
    link_table = selector(link_src, owned + received, state.dtype)

    def evaluate(current):
        flat_current = current.reshape(flat_rows, owned)
        packed = jnp.dot(flat_current, pack_table, precision=HIGHEST).reshape(
            2, sites, sites, received
        )
        commutator = commute(symmetric, current)
        total = jnp.stack([commutator[1], -commutator[0]]) - decay[None, None, None, :] * current
        moved = lax.all_to_all(packed, GRP_DEV, split_axis=3, concat_axis=3, tiled=True)
        combined = jnp.concatenate([flat_current, moved.reshape(flat_rows, received)], axis=1)
        fetched = jnp.dot(combined, link_table, precision=HIGHEST)
        for link in range(links):
            start = link * owned
            source = fetched[:, start : start + owned].reshape(2, sites, sites, owned)
            total = total + masked_term(source, link_site[link], link_coef[:, link])
        return total

    sections = [evaluate(state)]
    inner = state
    for weights in TABLEAU:
        inner = state
        for weight, section in zip(weights, sections):
            if weight != 0.0:
                inner = inner + step_size * weight * section
        sections.append(evaluate(inner))
    error = jnp.zeros_like(state)
    for weight, section in zip(ERRORS, sections):
        if weight != 0.0:
            error = error + step_size * weight * section
    scale = ABS_TOL + REL_TOL * jnp.maximum(jnp.abs(state), jnp.abs(inner))
    partial_sum = jnp.sum(jnp.square(error / scale))
    total_sum = one_axis_at_a_time(partial_sum, GRP_DEV)
    entries = 2 * sites * sites * owned * groups * members
    return (inner, jnp.sqrt(total_sum / entries))


def solution(mesh):
    finer = Mesh(
        mesh.devices.reshape(mesh.shape["grp"], 4, 4, 4), ("grp", "dev_0", "dev_1", "dev_2")
    )
    return jax.shard_map(
        shards,
        mesh=finer,
        in_specs=(
            P(None, None, None, GRP_DEV),
            P(),
            P(),
            P(None, GRP_DEV),
            P(None, GRP_DEV),
            P(None, GRP_DEV),
            P(None, None, GRP_DEV),
            P(GRP_DEV, None),
            P(),
        ),
        out_specs=(P(None, None, None, GRP_DEV), P()),
        check_vma=False,
    )
```

profile of v0, /device:TPU:0, one launch (start us, length us, event | category | flops | bytes accessed | tf_op | source)
XLA Modules:
  0.0 502.5 jit_solution(1082587879265455247)
XLA Ops:
  8.1 7.2 %reshape.4447 = f32[128,1,2304]{2,1,0:T(1,128)} reshape(f32[256,2,24,24]{3,2,1,0:T(8,128)} %bitcast.336) | data formatting | bytes 2359296
  15.4 11.3 %all-to-all-start = ((f32[128,1,2304]{2,1,0:T(1,128)}), f32[128,1,2304]{2,1,0:T(1,128)S(1)}, u32[]{:S(2)}, u32[]{:S(2)}) async-start(f32[128,1,2304]{2,1,0:T(1,128)} %reshape.4447), calls=%async_computation | async-start | bytes 2359296 | tf_op jit(solution)/shard_map/all_to_all | solution.py:83
  33.1 13.0 %all-to-all-done = f32[128,1,2304]{2,1,0:T(1,128)S(1)} async-done(((f32[128,1,2304]{2,1,0:T(1,128)}), f32[128,1,2304]{2,1,0:T(1,128)S(1)}, u32[]{:S(2)}, u32[]{:S(2)}) %all-to-all-start) | async-done | bytes 1179680 | tf_op jit(solution)/shard_map/all_to_all | solution.py:83
  75.5 7.2 %reshape.4449 = f32[128,1,2304]{2,1,0:T(1,128)} reshape(f32[256,2,24,24]{3,2,1,0:T(8,128)} %bitcast.338) | data formatting | bytes 2359296
  91.3 16.6 %all-to-all-done.1 = f32[128,1,2304]{2,1,0:T(1,128)} async-done(((f32[128,1,2304]{2,1,0:T(1,128)}), f32[128,1,2304]{2,1,0:T(1,128)}, u32[]{:S(2)}, u32[]{:S(2)}) %all-to-all-start.1) | async-done | bytes 1179680 | tf_op jit(solution)/shard_map/all_to_all | solution.py:83
  138.8 7.2 %reshape.4451 = f32[128,1,2304]{2,1,0:T(1,128)} reshape(f32[256,2,24,24]{3,2,1,0:T(8,128)} %bitcast.340) | data formatting | bytes 2359296
  154.5 16.6 %all-to-all-done.2 = f32[128,1,2304]{2,1,0:T(1,128)} async-done(((f32[128,1,2304]{2,1,0:T(1,128)}), f32[128,1,2304]{2,1,0:T(1,128)}, u32[]{:S(2)}, u32[]{:S(2)}) %all-to-all-start.2) | async-done | bytes 1179680 | tf_op jit(solution)/shard_map/all_to_all | solution.py:83
  201.4 7.2 %reshape.4453 = f32[128,1,2304]{2,1,0:T(1,128)} reshape(f32[256,2,24,24]{3,2,1,0:T(8,128)} %bitcast.342) | data formatting | bytes 2359296
  218.1 15.8 %all-to-all-done.3 = f32[128,1,2304]{2,1,0:T(1,128)} async-done(((f32[128,1,2304]{2,1,0:T(1,128)}), f32[128,1,2304]{2,1,0:T(1,128)}, u32[]{:S(2)}, u32[]{:S(2)}) %all-to-all-start.3) | async-done | bytes 1179680 | tf_op jit(solution)/shard_map/all_to_all | solution.py:83
  261.7 6.3 %copy.1048 = f32[2,24,24,256]{2,1,0,3:T(8,128)} copy(f32[2,24,24,256]{3,1,2,0:T(8,128)} %fusion.278) | data formatting | bytes 2359296 | tf_op jit(solution)/shard_map/dot_general | solution.py:78
  268.1 7.2 %reshape.4455 = f32[128,1,2304]{2,1,0:T(1,128)} reshape(f32[256,2,24,24]{3,2,1,0:T(8,128)} %bitcast.344) | data formatting | bytes 2359296
  283.8 16.6 %all-to-all-done.4 = f32[128,1,2304]{2,1,0:T(1,128)} async-done(((f32[128,1,2304]{2,1,0:T(1,128)}), f32[128,1,2304]{2,1,0:T(1,128)}, u32[]{:S(2)}, u32[]{:S(2)}) %all-to-all-start.4) | async-done | bytes 1179680 | tf_op jit(solution)/shard_map/all_to_all | solution.py:83
  306.2 6.7 %reshape.4456 = f32[256,2,24,24]{3,2,1,0:T(8,128)} reshape(f32[128,2304]{1,0:T(8,128)} %reduce.4) | data formatting | bytes 2359296
  330.9 6.3 %copy.1088 = f32[2,24,24,256]{2,1,0,3:T(8,128)} copy(f32[2,24,24,256]{3,1,2,0:T(8,128)} %fusion.276) | data formatting | bytes 2359296 | tf_op jit(solution)/shard_map/dot_general | solution.py:78
  337.3 7.2 %reshape.4457 = f32[128,1,2304]{2,1,0:T(1,128)} reshape(f32[256,2,24,24]{3,2,1,0:T(8,128)} %bitcast.346) | data formatting | bytes 2359296
  353.9 15.8 %all-to-all-done.5 = f32[128,1,2304]{2,1,0:T(1,128)} async-done(((f32[128,1,2304]{2,1,0:T(1,128)}), f32[128,1,2304]{2,1,0:T(1,128)}, u32[]{:S(2)}, u32[]{:S(2)}) %all-to-all-start.5) | async-done | bytes 1179680 | tf_op jit(solution)/shard_map/all_to_all | solution.py:83
  375.5 6.7 %reshape.4458 = f32[256,2,24,24]{3,2,1,0:T(8,128)} reshape(f32[128,2304]{1,0:T(8,128)} %reduce.5) | data formatting | bytes 2359296
  382.2 6.5 %copy.1089 = f32[2,24,24,256]{3,2,1,0:T(8,128)} copy(f32[2,24,24,256]{2,1,0,3:T(8,128)} %bitcast.347) | data formatting | bytes 2359296 | tf_op jit(solution)/shard_map/all_to_all | solution.py:83
  406.7 7.2 %reshape.4459 = f32[128,1,2304]{2,1,0:T(1,128)} reshape(f32[256,2,24,24]{3,2,1,0:T(8,128)} %bitcast.348) | data formatting | bytes 2359296
  422.4 16.6 %all-to-all-done.6 = f32[128,1,2304]{2,1,0:T(1,128)} async-done(((f32[128,1,2304]{2,1,0:T(1,128)}), f32[128,1,2304]{2,1,0:T(1,128)}, u32[]{:S(2)}, u32[]{:S(2)}) %all-to-all-start.6) | async-done | bytes 1179680 | tf_op jit(solution)/shard_map/all_to_all | solution.py:83
  444.8 6.7 %reshape.4460 = f32[256,2,24,24]{3,2,1,0:T(8,128)} reshape(f32[128,2304]{1,0:T(8,128)} %reduce.6) | data formatting | bytes 2359296
  470.9 9.9 %psum.29 = f32[]{:T(128)} all-reduce(f32[]{:T(128)} %psum.28), channel_id=1, replica_groups=mesh['grp'=2,'dev_0'=4,'dev_1'=4,'dev_2'=4] {'dev_0'}, use_global_device_ids=true, to_apply=%region_3.0 | all-reduce | flops 1 | bytes 8 | tf_op jit(solution)/shard_map/psum | solution.py:26
  480.8 9.7 %psum.30 = f32[]{:T(128)} all-reduce(f32[]{:T(128)} %psum.29), channel_id=1, replica_groups=mesh['grp'=2,'dev_0'=4,'dev_1'=4,'dev_2'=4] {'dev_1'}, use_global_device_ids=true, to_apply=%region_4.0 | all-reduce | flops 1 | bytes 8 | tf_op jit(solution)/shard_map/psum | solution.py:26
  490.5 10.0 %psum.31 = f32[]{:T(128)} all-reduce(f32[]{:T(128)} %psum.30), channel_id=1, replica_groups=mesh['grp'=2,'dev_0'=4,'dev_1'=4,'dev_2'=4] {'dev_2'}, use_global_device_ids=true, to_apply=%region_5.0 | all-reduce | flops 1 | bytes 8 | tf_op jit(solution)/shard_map/psum | solution.py:26
  (687 shorter events, 254.4 us)
Async XLA Ops:
  15.4 11.4 %copy-start.263 = (f32[4,8,128]{2,1,0:T(8,128)S(1)}, f32[4,8,128]{2,1,0:T(8,128)}, u32[]{:S(2)}) copy-start(f32[4,8,128]{2,1,0:T(8,128)} %param.15) | copy-start | bytes 49156
  15.4 12.1 %copy-start.264 = (s32[8,128]{1,0:T(8,128)S(1)}, s32[8,128]{1,0:T(8,128)}, u32[]{:S(2)}) copy-start(s32[8,128]{1,0:T(8,128)} %param.14) | copy-start | bytes 12292
  15.4 12.1 %copy-start.255 = (f32[24,24]{1,0:T(8,128)S(1)}, f32[24,24]{1,0:T(8,128)}, u32[]{:S(2)}) copy-start(f32[24,24]{1,0:T(8,128)} %param.10) | copy-start | bytes 6916
  15.4 12.2 %copy-start.266 = (f32[96]{0:T(128)S(1)}, f32[96]{0:T(128)}, u32[]{:S(2)}) copy-start(f32[96]{0:T(128)} %param.11) | copy-start | bytes 1156
  15.4 12.3 %copy-start.265 = (s32[3,128]{1,0:T(4,128)S(1)}, s32[3,128]{1,0:T(4,128)}, u32[]{:S(2)}) copy-start(s32[3,128]{1,0:T(4,128)} %param.12) | copy-start | bytes 4612
  15.4 15.5 %copy-start = (f32[2,24,24,128]{3,2,1,0:T(8,128)S(1)}, f32[2,24,24,128]{3,2,1,0:T(8,128)}, u32[]{:S(2)}) copy-start(f32[2,24,24,128]{3,2,1,0:T(8,128)} %param.9) | copy-start | bytes 1769476
  15.4 30.7 %all-to-all-start = ((f32[128,1,2304]{2,1,0:T(1,128)}), f32[128,1,2304]{2,1,0:T(1,128)S(1)}, u32[]{:S(2)}, u32[]{:S(2)}) async-start(f32[128,1,2304]{2,1,0:T(1,128)} %reshape.4447), calls=%async_computation | async-start | bytes 2359296 | tf_op jit(solution)/shard_map/all_to_all | solution.py:83
  56.4 5.3 %copy-start.248 = (s32[8,128]{1,0:T(8,128)S(1)}, s32[8,128]{1,0:T(8,128)}, u32[]{:S(2)}) copy-start(s32[8,128]{1,0:T(8,128)} %param.13) | copy-start | bytes 12292
  82.7 25.2 %all-to-all-start.1 = ((f32[128,1,2304]{2,1,0:T(1,128)}), f32[128,1,2304]{2,1,0:T(1,128)}, u32[]{:S(2)}, u32[]{:S(2)}) async-start(f32[128,1,2304]{2,1,0:T(1,128)} %reshape.4449), calls=%async_computation.1 | async-start | bytes 2359296 | tf_op jit(solution)/shard_map/all_to_all | solution.py:83
  146.0 25.1 %all-to-all-start.2 = ((f32[128,1,2304]{2,1,0:T(1,128)}), f32[128,1,2304]{2,1,0:T(1,128)}, u32[]{:S(2)}, u32[]{:S(2)}) async-start(f32[128,1,2304]{2,1,0:T(1,128)} %reshape.4451), calls=%async_computation.2 | async-start | bytes 2359296 | tf_op jit(solution)/shard_map/all_to_all | solution.py:83
  208.7 25.2 %all-to-all-start.3 = ((f32[128,1,2304]{2,1,0:T(1,128)}), f32[128,1,2304]{2,1,0:T(1,128)}, u32[]{:S(2)}, u32[]{:S(2)}) async-start(f32[128,1,2304]{2,1,0:T(1,128)} %reshape.4453), calls=%async_computation.3 | async-start | bytes 2359296 | tf_op jit(solution)/shard_map/all_to_all | solution.py:83
  275.3 25.1 %all-to-all-start.4 = ((f32[128,1,2304]{2,1,0:T(1,128)}), f32[128,1,2304]{2,1,0:T(1,128)}, u32[]{:S(2)}, u32[]{:S(2)}) async-start(f32[128,1,2304]{2,1,0:T(1,128)} %reshape.4455), calls=%async_computation.4 | async-start | bytes 2359296 | tf_op jit(solution)/shard_map/all_to_all | solution.py:83
  326.3 1.3 copy-start.12
  326.3 1.4 copy-start.13
  326.3 1.4 copy-start.260
  327.7 1.5 copy-start.253
  344.5 25.2 %all-to-all-start.5 = ((f32[128,1,2304]{2,1,0:T(1,128)}), f32[128,1,2304]{2,1,0:T(1,128)}, u32[]{:S(2)}, u32[]{:S(2)}) async-start(f32[128,1,2304]{2,1,0:T(1,128)} %reshape.4457), calls=%async_computation.5 | async-start | bytes 2359296 | tf_op jit(solution)/shard_map/all_to_all | solution.py:83
  382.2 6.5 %copy-start.9 = (f32[2,24,24,128]{3,2,1,0:T(8,128)S(1)}, f32[2,24,24,128]{3,2,1,0:T(8,128)}, u32[]{:S(2)}) copy-start(f32[2,24,24,128]{3,2,1,0:T(8,128)} %copy.1084) | copy-start | bytes 1769476
  397.2 1.5 copy-start.254
  413.9 25.1 %all-to-all-start.6 = ((f32[128,1,2304]{2,1,0:T(1,128)}), f32[128,1,2304]{2,1,0:T(1,128)}, u32[]{:S(2)}, u32[]{:S(2)}) async-start(f32[128,1,2304]{2,1,0:T(1,128)} %reshape.4459), calls=%async_computation.6 | async-start | bytes 2359296 | tf_op jit(solution)/shard_map/all_to_all | solution.py:83
  420.2 37.6 %copy-start.7 = (f32[2,24,24,128]{3,2,1,0:T(8,128)}, f32[2,24,24,128]{3,2,1,0:T(8,128)S(1)}, u32[]{:S(2)}) copy-start(f32[2,24,24,128]{3,2,1,0:T(8,128)S(1)} %copy.1162) | copy-start | bytes 1769476
  465.0 1.3 copy-start.10
  465.0 1.4 copy-start.11
  465.0 1.4 copy-start.262
  (250 other events, 196.8 us)
where the time goes:
time: 509 us; the launch traced here: 503 us
  local copies, waits for them, and re-layouts  194 us (38%)
  waiting for transfers between devices  111 us (22%)
  other arithmetic  59.6 us (12%)
  matrix products  50.3 us (10%)
  starting transfers between devices  48.3 us (9%)
  blocking collectives  32.6 us (6%)
  between operations  6.24 us (1%)
    all_to_all x7, waiting for transfers between devices, evaluate(): lax.all_to_all(packed, GRP_DEV, split_axis=3, concat_axis=3, tiled=True)  111 us
    unnamed x550, local copies, waits for them, and re-layouts  107 us
    all_to_all x7, starting transfers between devices, evaluate(): lax.all_to_all(packed, GRP_DEV, split_axis=3, concat_axis=3, tiled=True)  48.3 us
    all_to_all x8, local copies, waits for them, and re-layouts, evaluate(): lax.all_to_all(packed, GRP_DEV, split_axis=3, concat_axis=3, tiled=True)  41 us
    dot_general x7, local copies, waits for them, and re-layouts, evaluate(): jnp.dot(flat_current, pack_table, precision=HIGHEST)  35.6 us
    all_to_all x7, other arithmetic, evaluate(): lax.all_to_all(packed, GRP_DEV, split_axis=3, concat_axis=3, tiled=True)  34.9 us
    psum x4, blocking collectives, one_axis_at_a_time(): return functools.reduce(lax.psum, axes, shard)  32.6 us
    dot_general x7, matrix products, evaluate(): fetched = jnp.dot(combined, link_table, precision=HIGHEST)  32.2 us
  transfers between devices with their start and end apart: 7, of which 7 were waited for; matrix products, arithmetic and copies ran while one was open for 4% of the time, Pallas kernels for 0%

commit v1 on v0

--- a/solution.py
+++ b/solution.py
@@ -80,7 +80,12 @@
         )
         commutator = commute(symmetric, current)
         total = jnp.stack([commutator[1], -commutator[0]]) - decay[None, None, None, :] * current
-        moved = lax.all_to_all(packed, GRP_DEV, split_axis=3, concat_axis=3, tiled=True)
+        moved = jnp.concatenate(
+            lax.all_to_all(
+                jnp.stack(jnp.split(packed, lax.axis_size(GRP_DEV), axis=3)), GRP_DEV, 0, 0
+            ),
+            axis=3,
+        )
         combined = jnp.concatenate([flat_current, moved.reshape(flat_rows, received)], axis=1)
         fetched = jnp.dot(combined, link_table, precision=HIGHEST)
         for link in range(links):

time: 509 us -> 1860 us (3.65)
  local copies, waits for them, and re-layouts: 194 us -> 1480 us
  other arithmetic: 59.6 us -> 111 us
    unnamed x550 -> x927, local copies, waits for them, and re-layouts: 107 us -> 1030 us
    another operation x0 -> x21, local copies, waits for them, and re-layouts: none -> 393 us  [the longest x14 352 us: evaluate(): jnp.stack(jnp.split(packed, lax.axis_size(GRP_DEV), axis=3))]
    reshape x1 -> x21, local copies, waits for them, and re-layouts: 5.35 us -> 52.5 us  [the longest x14 45 us: evaluate(): jnp.concatenate(lax.all_to_all(jnp.stack(jnp.split(packed, lax.axis_size(...]
    add x56, other arithmetic: 7.37 us -> 49.8 us  [masked_term(): imag_part = weight_real * source[1] + weight_imag * source[0]]
    all_to_all x8 -> x1, local copies, waits for them, and re-layouts: 41 us -> 0.51 us  [evaluate(): lax.all_to_all(jnp.stack(jnp.split(packed, lax.axis_size(GRP_DEV), axis=3...]
    dot_general x7 -> x1, local copies, waits for them, and re-layouts: 35.6 us -> 0.36 us  [evaluate(): jnp.dot(flat_current, pack_table, precision=HIGHEST)]
  transfers between devices with their start and end apart: 7 -> 7, of which waited for: 7 -> 7; matrix products, arithmetic and copies ran while one was open for 4% -> 1% of each run, Pallas kernels for 0% -> 0%
where the time goes in v1:
time: 1860 us; the launch traced here: 1840 us
  local copies, waits for them, and re-layouts  1480 us (80%)
  other arithmetic  111 us (6%)
  waiting for transfers between devices  106 us (6%)
  matrix products  55.2 us (3%)
  starting transfers between devices  47.4 us (3%)
  blocking collectives  32.6 us (2%)
    unnamed x927, local copies, waits for them, and re-layouts  1030 us
    another operation x14, local copies, waits for them, and re-layouts, evaluate(): jnp.stack(jnp.split(packed, lax.axis_size(GRP_DEV), axis=3))  352 us
    all_to_all x7, waiting for transfers between devices, evaluate(): lax.all_to_all(jnp.stack(jnp.split(packed, lax.axis_size(GRP_DEV), axis=3...  106 us
    add x56, other arithmetic, masked_term(): imag_part = weight_real * source[1] + weight_imag * source[0]  49.8 us
    all_to_all x7, starting transfers between devices, evaluate(): lax.all_to_all(jnp.stack(jnp.split(packed, lax.axis_size(GRP_DEV), axis=3...  47.4 us
    reshape x14, local copies, waits for them, and re-layouts, evaluate(): jnp.concatenate(lax.all_to_all(jnp.stack(jnp.split(packed, lax.axis_size(...  45 us
    another operation x7, local copies, waits for them, and re-layouts, evaluate(): moved.reshape(flat_rows, received)  41.3 us
  transfers between devices with their start and end apart: 7, of which 7 were waited for; matrix products, arithmetic and copies ran while one was open for 1% of the time, Pallas kernels for 0%

profile of v1, /device:TPU:0, one launch (start us, length us, event | category | flops | bytes accessed | tf_op | source)
XLA Modules:
  0.0 1835.9 jit_solution(9199271345323218784)
XLA Ops:
  136.8 49.2 %copy.1804 = f32[128,2,24,24,2]{3,2,4,1,0:T(8,128)} copy(f32[128,2,24,24,2]{4,3,2,1,0:T(8,128)} %constant_dynamic-update-slice_fusion) | data formatting | bytes 2359296 | tf_op jit(solution)/shard_map/stack | solution.py:85
  186.0 7.2 reshape.4447
  193.2 11.6 all-to-all-start
  212.3 11.9 all-to-all-done
  396.0 49.2 %copy.1847 = f32[128,2,24,24,2]{3,2,4,1,0:T(8,128)} copy(f32[128,2,24,24,2]{4,3,2,1,0:T(8,128)} %constant_dynamic-update-slice_fusion.128) | data formatting | bytes 2359296 | tf_op jit(solution)/shard_map/stack | solution.py:85
  445.2 7.2 reshape.4449
  461.7 15.6 all-to-all-done.1
  650.9 49.2 %copy.1887 = f32[128,2,24,24,2]{3,2,4,1,0:T(8,128)} copy(f32[128,2,24,24,2]{4,3,2,1,0:T(8,128)} %constant_dynamic-update-slice_fusion.256) | data formatting | bytes 2359296 | tf_op jit(solution)/shard_map/stack | solution.py:85
  700.1 7.2 reshape.4451
  716.8 15.6 all-to-all-done.2
  904.9 49.2 %copy.1928 = f32[128,2,24,24,2]{3,2,4,1,0:T(8,128)} copy(f32[128,2,24,24,2]{4,3,2,1,0:T(8,128)} %constant_dynamic-update-slice_fusion.384) | data formatting | bytes 2359296 | tf_op jit(solution)/shard_map/stack | solution.py:85
  954.1 7.2 reshape.4453
  970.8 15.5 all-to-all-done.3
  1162.7 49.2 %copy.1969 = f32[128,2,24,24,2]{3,2,4,1,0:T(8,128)} copy(f32[128,2,24,24,2]{4,3,2,1,0:T(8,128)} %constant_dynamic-update-slice_fusion.512) | data formatting | bytes 2359296 | tf_op jit(solution)/shard_map/stack | solution.py:85
  1211.9 7.2 reshape.4455
  1228.6 15.5 all-to-all-done.4
  1420.7 49.2 %copy.2010 = f32[128,2,24,24,2]{3,2,4,1,0:T(8,128)} copy(f32[128,2,24,24,2]{4,3,2,1,0:T(8,128)} %constant_dynamic-update-slice_fusion.640) | data formatting | bytes 2359296 | tf_op jit(solution)/shard_map/stack | solution.py:85
  1469.8 7.2 reshape.4457
  1486.5 15.6 all-to-all-done.5
  1678.7 49.2 %copy.2050 = f32[128,2,24,24,2]{3,2,4,1,0:T(8,128)} copy(f32[128,2,24,24,2]{4,3,2,1,0:T(8,128)} %constant_dynamic-update-slice_fusion.768) | data formatting | bytes 2359296 | tf_op jit(solution)/shard_map/stack | solution.py:85
  1743.6 16.5 all-to-all-done.6
  1804.1 9.8 psum.29
  1813.9 9.8 psum.30
  1823.8 9.9 psum.31
  (1092 shorter events, 1296.0 us)
Async XLA Ops:
  84.2 120.6 %copy-start = (f32[2,24,24,128]{3,2,1,0:T(8,128)S(1)}, f32[2,24,24,128]{3,2,1,0:T(8,128)}, u32[]{:S(2)}) copy-start(f32[2,24,24,128]{3,2,1,0:T(8,128)} %param.9) | copy-start | bytes 1769476
  85.3 120.6 %copy-start.7 = (f32[4,8,128]{2,1,0:T(8,128)S(1)}, f32[4,8,128]{2,1,0:T(8,128)}, u32[]{:S(2)}) copy-start(f32[4,8,128]{2,1,0:T(8,128)} %param.15) | copy-start | bytes 49156
  85.3 121.3 %copy-start.8 = (s32[8,128]{1,0:T(8,128)S(1)}, s32[8,128]{1,0:T(8,128)}, u32[]{:S(2)}) copy-start(s32[8,128]{1,0:T(8,128)} %param.14) | copy-start | bytes 12292
  85.3 121.3 %copy-start.6 = (f32[24,24]{1,0:T(8,128)S(1)}, f32[24,24]{1,0:T(8,128)}, u32[]{:S(2)}) copy-start(f32[24,24]{1,0:T(8,128)} %param.10) | copy-start | bytes 6916
  85.3 121.4 %copy-start.10 = (f32[96]{0:T(128)S(1)}, f32[96]{0:T(128)}, u32[]{:S(2)}) copy-start(f32[96]{0:T(128)} %param.11) | copy-start | bytes 1156
  85.3 121.5 %copy-start.9 = (s32[3,128]{1,0:T(4,128)S(1)}, s32[3,128]{1,0:T(4,128)}, u32[]{:S(2)}) copy-start(s32[3,128]{1,0:T(4,128)} %param.12) | copy-start | bytes 4612
  127.3 118.8 %copy-start.5 = (s32[8,128]{1,0:T(8,128)S(1)}, s32[8,128]{1,0:T(8,128)}, u32[]{:S(2)}) copy-start(s32[8,128]{1,0:T(8,128)} %param.13) | copy-start | bytes 12292
  193.2 30.9 %all-to-all-start = ((f32[128,1,2304]{2,1,0:T(1,128)}), f32[128,1,2304]{2,1,0:T(1,128)S(1)}, u32[]{:S(2)}, u32[]{:S(2)}) async-start(f32[128,1,2304]{2,1,0:T(1,128)} %reshape.4447), calls=%async_computation | async-start | bytes 2359296 | tf_op jit(solution)/shard_map/all_to_all | solution.py:84
  452.4 25.0 %all-to-all-start.1 = ((f32[128,1,2304]{2,1,0:T(1,128)}), f32[128,1,2304]{2,1,0:T(1,128)}, u32[]{:S(2)}, u32[]{:S(2)}) async-start(f32[128,1,2304]{2,1,0:T(1,128)} %reshape.4449), calls=%async_computation.1 | async-start | bytes 2359296 | tf_op jit(solution)/shard_map/all_to_all | solution.py:84
  650.9 116.8 %copy-start.2 = (f32[2,24,24,128]{3,1,2,0:T(8,128)S(1)}, f32[2,24,24,128]{3,1,2,0:T(8,128)}, u32[]{:S(2)}) copy-start(f32[2,24,24,128]{3,1,2,0:T(8,128)} %get-tuple-element.21) | copy-start | bytes 1769476
  707.4 25.0 %all-to-all-start.2 = ((f32[128,1,2304]{2,1,0:T(1,128)}), f32[128,1,2304]{2,1,0:T(1,128)}, u32[]{:S(2)}, u32[]{:S(2)}) async-start(f32[128,1,2304]{2,1,0:T(1,128)} %reshape.4451), calls=%async_computation.2 | async-start | bytes 2359296 | tf_op jit(solution)/shard_map/all_to_all | solution.py:84
  904.9 119.8 %copy-start.3 = (f32[2,24,24,128]{3,1,2,0:T(8,128)S(1)}, f32[2,24,24,128]{3,1,2,0:T(8,128)}, u32[]{:S(2)}) copy-start(f32[2,24,24,128]{3,1,2,0:T(8,128)} %get-tuple-element.21) | copy-start | bytes 1769476
  961.3 25.0 %all-to-all-start.3 = ((f32[128,1,2304]{2,1,0:T(1,128)}), f32[128,1,2304]{2,1,0:T(1,128)}, u32[]{:S(2)}, u32[]{:S(2)}) async-start(f32[128,1,2304]{2,1,0:T(1,128)} %reshape.4453), calls=%async_computation.3 | async-start | bytes 2359296 | tf_op jit(solution)/shard_map/all_to_all | solution.py:84
  1162.7 119.5 %copy-start.1 = (f32[2,24,24,128]{3,1,2,0:T(8,128)S(1)}, f32[2,24,24,128]{3,1,2,0:T(8,128)}, u32[]{:S(2)}) copy-start(f32[2,24,24,128]{3,1,2,0:T(8,128)} %get-tuple-element.17) | copy-start | bytes 1769476
  1219.1 25.0 %all-to-all-start.4 = ((f32[128,1,2304]{2,1,0:T(1,128)}), f32[128,1,2304]{2,1,0:T(1,128)}, u32[]{:S(2)}, u32[]{:S(2)}) async-start(f32[128,1,2304]{2,1,0:T(1,128)} %reshape.4455), calls=%async_computation.4 | async-start | bytes 2359296 | tf_op jit(solution)/shard_map/all_to_all | solution.py:84
  1477.1 25.0 %all-to-all-start.5 = ((f32[128,1,2304]{2,1,0:T(1,128)}), f32[128,1,2304]{2,1,0:T(1,128)}, u32[]{:S(2)}, u32[]{:S(2)}) async-start(f32[128,1,2304]{2,1,0:T(1,128)} %reshape.4457), calls=%async_computation.5 | async-start | bytes 2359296 | tf_op jit(solution)/shard_map/all_to_all | solution.py:84
  1543.2 199.0 %copy-start.4 = (f32[2,24,24,128]{3,2,1,0:T(8,128)}, f32[2,24,24,128]{3,2,1,0:T(8,128)S(1)}, u32[]{:S(2)}) copy-start(f32[2,24,24,128]{3,2,1,0:T(8,128)S(1)} %copy.2086) | copy-start | bytes 1769476
  1735.1 25.0 %all-to-all-start.6 = ((f32[128,1,2304]{2,1,0:T(1,128)}), f32[128,1,2304]{2,1,0:T(1,128)}, u32[]{:S(2)}, u32[]{:S(2)}) async-start(f32[128,1,2304]{2,1,0:T(1,128)} %reshape.4459), calls=%async_computation.6 | async-start | bytes 2359296 | tf_op jit(solution)/shard_map/all_to_all | solution.py:84
